TPU v7x, 32 devices: a whole 2x2x4 slice. The times are simulated.
32 devices in a mesh: dp: 4 (over z), seq: 2 (over x), tensor: 4 (over y, core).
Axes of the slice: x: 2, y: 2, z: 4, core: 2. Of those that a mesh axis runs over, the one named last changes fastest.
Arguments:
- latents: bfloat16 [4, 4, 256, 1152], P('dp', 'seq', 'tensor'), may hold values from -6 to 6
- modulation: float32 [4, 6, 1152], P('dp'), may hold values from -3 to 3
- in_weight: bfloat16 [1152, 3, 1152], P(None, None, 'tensor'), may hold values from -0.5 to 0.5
- out_weight: bfloat16 [1152, 1152], P('tensor'), may hold values from -0.1875 to 0.1875
- up_weight: bfloat16 [1152, 4608], P(None, 'tensor'), may hold values from -0.1875 to 0.1875
- down_weight: bfloat16 [4608, 1152], P('tensor'), may hold values from -0.09375 to 0.09375
- cotangent: bfloat16 [4, 4, 256, 1152], P('dp', 'seq', 'tensor'), may hold values from -6 to 6
Outputs:
- result: bfloat16 [4, 4, 256, 1152], P('dp', 'seq', 'tensor')
- latents_grad: bfloat16 [4, 4, 256, 1152], P('dp', 'seq', 'tensor')
- in_grad: bfloat16 [1152, 3, 1152], P(('dp', 'seq'), None, 'tensor')
- out_grad: bfloat16 [1152, 1152], P('tensor', ('dp', 'seq'))
- up_grad: bfloat16 [1152, 4608], P(('dp', 'seq'), 'tensor')
- down_grad: bfloat16 [4608, 1152], P('tensor', ('dp', 'seq'))
All inputs are finite; a program needn't handle non-finite values.
Results may differ from a plain program's by a relative error of at most 0.02.
The roundings to bfloat16 on the way count: a program that leaves them out, or rounds other values in their place, can miss the bound.
Values may be sent and summed in bfloat16 or wider, within the bound.
A program may use at most 128 MiB of HBM per device.

v0:
```python
import math

import jax
import jax.numpy as jnp
from jax import lax
from jax.sharding import PartitionSpec as P

HEAD_DIM = 72


epsilon = 1e-06


def normalize(rows):
    center = jnp.mean(rows, axis=-1, keepdims=True)
    centred = rows - center
    spread = jnp.mean(centred * centred, axis=-1, keepdims=True)
    inverse = lax.rsqrt(spread + epsilon)
    return (centred * inverse, inverse)


def norm_back(normed, inverse, upstream):
    mean_grad = jnp.mean(upstream, axis=-1, keepdims=True)
    mean_cross = jnp.mean(upstream * normed, axis=-1, keepdims=True)
    return (upstream - mean_grad - normed * mean_cross) * inverse


def gelu_tanh(values):
    return jax.nn.gelu(values, approximate=True)


def flat_dot(left, right):
    leading = left.shape[:-1]
    out_rows = jnp.dot(left.reshape(-1, left.shape[-1]), right, preferred_element_type=jnp.float32)
    return out_rows.reshape(leading + (right.shape[-1],))


def flat_dot_t(left, right):
    leading = left.shape[:-1]
    out_rows = lax.dot_general(
        left.reshape(-1, left.shape[-1]),
        right,
        (((1,), (1,)), ((), ())),
        preferred_element_type=jnp.float32,
    )
    return out_rows.reshape(leading + (right.shape[0],))


def weight_grad(left, right):
    return lax.dot_general(
        left.reshape(-1, left.shape[-1]),
        right.reshape(-1, right.shape[-1]),
        (((0,), (0,)), ((), ())),
        preferred_element_type=jnp.float32,
    )


def attend(queries, key_rows, value_rows):
    scaling = 1.0 / math.sqrt(queries.shape[-1])
    scores = (
        jnp.einsum("bfphe,bgphe->bphfg", queries, key_rows, preferred_element_type=jnp.float32)
        * scaling
    )
    highest = jnp.max(scores, axis=-1, keepdims=True)
    raised = jnp.exp(scores - highest)
    probs = raised / jnp.sum(raised, axis=-1, keepdims=True)
    probs_low = probs.astype(jnp.bfloat16)
    attended = jnp.einsum(
        "bphfg,bgphe->bfphe", probs_low, value_rows, preferred_element_type=jnp.float32
    ).astype(jnp.bfloat16)
    return (attended, probs, probs_low)


def attend_back(queries, key_rows, value_rows, probs, probs_low, attended_grad):
    scaling = 1.0 / math.sqrt(queries.shape[-1])
    value_grad = jnp.einsum(
        "bphfg,bfphe->bgphe", probs_low, attended_grad, preferred_element_type=jnp.float32
    ).astype(jnp.bfloat16)
    prob_grad = jnp.einsum(
        "bfphe,bgphe->bphfg", attended_grad, value_rows, preferred_element_type=jnp.float32
    )
    score_grad = probs * (prob_grad - jnp.sum(probs * prob_grad, axis=-1, keepdims=True)) * scaling
    score_low = score_grad.astype(jnp.bfloat16)
    query_grad = jnp.einsum(
        "bphfg,bgphe->bfphe", score_low, key_rows, preferred_element_type=jnp.float32
    ).astype(jnp.bfloat16)
    key_grad = jnp.einsum(
        "bphfg,bfphe->bgphe", score_low, queries, preferred_element_type=jnp.float32
    ).astype(jnp.bfloat16)
    return (query_grad, key_grad, value_grad)


def body(latents, modulation, in_weight, out_weight, up_weight, down_weight, cotangent):
    width = latents.shape[-1]
    local_width = out_weight.shape[0]
    heads_here = local_width // HEAD_DIM
    modulate = modulation[:, :, None, None, :]
    shift_first, scale_first, gate_first = (modulate[:, 0], modulate[:, 1], modulate[:, 2])
    shift_second, scale_second, gate_second = (modulate[:, 3], modulate[:, 4], modulate[:, 5])
    inputs = latents.astype(jnp.float32)
    first_normed, first_inverse = normalize(inputs)
    first_input = (first_normed * (1.0 + scale_first) + shift_first).astype(jnp.bfloat16)
    first_full = lax.all_gather(first_input, "tensor", axis=2, tiled=True)
    in_flat = in_weight.reshape(width, 3 * local_width)
    projected = flat_dot(first_full, in_flat).astype(jnp.bfloat16)
    by_pixel = lax.all_to_all(projected, "seq", split_axis=2, concat_axis=1, tiled=True)
    samples, frames_all, pixel_part = (by_pixel.shape[0], by_pixel.shape[1], by_pixel.shape[2])
    split_parts = by_pixel.reshape(samples, frames_all, pixel_part, 3, heads_here, HEAD_DIM)
    queries, key_rows, value_rows = (
        split_parts[:, :, :, 0],
        split_parts[:, :, :, 1],
        split_parts[:, :, :, 2],
    )
    attended, probs, probs_low = attend(queries, key_rows, value_rows)
    attended_pix = attended.reshape(samples, frames_all, pixel_part, local_width)
    attended_rows = lax.all_to_all(attended_pix, "seq", split_axis=1, concat_axis=2, tiled=True)
    attention = lax.psum_scatter(
        flat_dot(attended_rows, out_weight).astype(jnp.bfloat16),
        "tensor",
        scatter_dimension=2,
        tiled=True,
    ).astype(jnp.float32)
    midway = inputs + gate_first * attention
    second_normed, second_inverse = normalize(midway)
    second_input = (second_normed * (1.0 + scale_second) + shift_second).astype(jnp.bfloat16)
    second_full = lax.all_gather(second_input, "tensor", axis=2, tiled=True)
    hidden = flat_dot(second_full, up_weight)
    activated = gelu_tanh(hidden).astype(jnp.bfloat16)
    feedforward = lax.psum_scatter(
        flat_dot(activated, down_weight).astype(jnp.bfloat16),
        "tensor",
        scatter_dimension=2,
        tiled=True,
    ).astype(jnp.float32)
    result = (midway + gate_second * feedforward).astype(jnp.bfloat16)
    upstream = cotangent.astype(jnp.float32)
    branch_grad = (gate_second * upstream).astype(jnp.bfloat16)
    branch_full = lax.all_gather(branch_grad, "tensor", axis=2, tiled=True)
    down_local = weight_grad(activated, branch_full)
    activated_grad = flat_dot_t(branch_full, down_weight)
    hidden_grad = jax.vjp(gelu_tanh, hidden)[1](activated_grad)[0].astype(jnp.bfloat16)
    up_local = weight_grad(second_full, hidden_grad)
    second_grad = lax.psum_scatter(
        flat_dot_t(hidden_grad, up_weight).astype(jnp.bfloat16),
        "tensor",
        scatter_dimension=2,
        tiled=True,
    ).astype(jnp.float32)
    midway_grad = upstream + norm_back(
        second_normed, second_inverse, second_grad * (1.0 + scale_second)
    )
    attention_grad = (gate_first * midway_grad).astype(jnp.bfloat16)
    attention_full = lax.all_gather(attention_grad, "tensor", axis=2, tiled=True)
    out_local = weight_grad(attended_rows, attention_full)
    attended_grad = flat_dot_t(attention_full, out_weight).astype(jnp.bfloat16)
    grad_pixels = lax.all_to_all(attended_grad, "seq", split_axis=2, concat_axis=1, tiled=True)
    grad_pixels = grad_pixels.reshape(samples, frames_all, pixel_part, heads_here, HEAD_DIM)
    query_grad, key_grad, value_grad = attend_back(
        queries, key_rows, value_rows, probs, probs_low, grad_pixels
    )
    stacked_grad = jnp.stack([query_grad, key_grad, value_grad], axis=3).reshape(
        samples, frames_all, pixel_part, 3 * local_width
    )
    projected_grad = lax.all_to_all(stacked_grad, "seq", split_axis=1, concat_axis=2, tiled=True)
    in_local = weight_grad(first_full, projected_grad).reshape(width, 3, local_width)
    first_grad = lax.psum_scatter(
        flat_dot_t(projected_grad, in_flat).astype(jnp.bfloat16),
        "tensor",
        scatter_dimension=2,
        tiled=True,
    ).astype(jnp.float32)
    latents_grad = (
        midway_grad + norm_back(first_normed, first_inverse, first_grad * (1.0 + scale_first))
    ).astype(jnp.bfloat16)
    col_groups = (
        lax.psum_scatter(
            down_local.astype(jnp.bfloat16), "dp", scatter_dimension=1, tiled=True
        ).astype(jnp.float32),
        lax.psum_scatter(
            out_local.astype(jnp.bfloat16), "dp", scatter_dimension=1, tiled=True
        ).astype(jnp.float32),
    )
    down_local, out_local = (
        lax.psum_scatter(
            col_groups[0].astype(jnp.bfloat16), "seq", scatter_dimension=1, tiled=True
        ).astype(jnp.float32),
        lax.psum_scatter(
            col_groups[1].astype(jnp.bfloat16), "seq", scatter_dimension=1, tiled=True
        ).astype(jnp.float32),
    )
    row_groups = (
        lax.psum_scatter(
            up_local.astype(jnp.bfloat16), "dp", scatter_dimension=0, tiled=True
        ).astype(jnp.float32),
        lax.psum_scatter(
            in_local.astype(jnp.bfloat16), "dp", scatter_dimension=0, tiled=True
        ).astype(jnp.float32),
    )
    up_local, in_local = (
        lax.psum_scatter(
            row_groups[0].astype(jnp.bfloat16), "seq", scatter_dimension=0, tiled=True
        ).astype(jnp.float32),
        lax.psum_scatter(
            row_groups[1].astype(jnp.bfloat16), "seq", scatter_dimension=0, tiled=True
        ).astype(jnp.float32),
    )
    return (
        result,
        latents_grad,
        in_local.astype(jnp.bfloat16),
        out_local.astype(jnp.bfloat16),
        up_local.astype(jnp.bfloat16),
        down_local.astype(jnp.bfloat16),
    )


def solution(mesh):
    placed = (
        P("dp", "seq", "tensor", None),
        P("dp", None, None),
        P(None, None, "tensor"),
        P("tensor", None),
        P(None, "tensor"),
        P("tensor", None),
        P("dp", "seq", "tensor", None),
    )
    return jax.shard_map(
        body,
        mesh=mesh,
        in_specs=placed,
        out_specs=(
            P("dp", "seq", "tensor", None),
            P("dp", "seq", "tensor", None),
            P(("dp", "seq"), None, "tensor"),
            P("tensor", ("dp", "seq")),
            P(("dp", "seq"), "tensor"),
            P("tensor", ("dp", "seq")),
        ),
        check_vma=False,
    )
```

profile of v0, /device:TPU:0, one launch (start us, length us, event | category | flops | bytes accessed | tf_op | source)
XLA Modules:
  0.0 533.6 jit_solution(3522003502128376436)
XLA Ops:
  13.1 20.3 %all-gather.5.cloned.1.call-done = bf16[1,2,256,1152]{3,2,1,0:T(8,128)(2,1)} async-done(((bf16[1,2,64,1152]{3,2,1,0:T(8,128)(2,1)}), bf16[1,2,256,1152]{3,2,1,0:T(8,128)(2,1)}) %all-gather.5.cloned.1.call-update) | async-done | bytes 1179664 | tf_op jit(solution)/shard_map/all_gather | solution.py:103
  41.3 16.4 %all_to_all.60 = bf16[1,2,256,864]{3,1,0,2:T(2,128)(2,1)S(1)} all-to-all(bf16[1,2,256,864]{3,1,0,2:T(2,128)(2,1)} %copy.61), channel_id=1, replica_groups=mesh['dp'=4,'seq'=2,'tensor'=4] {'seq'}, dimensions={2} | all-to-all | bytes 1769472 | tf_op jit(solution)/shard_map/all_to_all | solution.py:106
  73.6 7.7 %all_to_all.61 = bf16[1,4,128,288]{2,3,0,1:T(8,128)(2,1)S(1)} all-to-all(bf16[1,4,128,288]{2,3,0,1:T(8,128)(2,1)S(1)} %bitcast.170), channel_id=1, replica_groups=mesh['dp'=4,'seq'=2,'tensor'=4] {'seq'}, dimensions={1} | all-to-all | bytes 589824 | tf_op jit(solution)/shard_map/all_to_all | solution.py:116
  87.0 23.9 %reduce-scatter.17.cloned.1.call-done = bf16[1,2,64,1152]{3,2,1,0:T(8,128)(2,1)} async-done(((bf16[1,2,256,1152]{3,2,1,0:T(8,128)(2,1)}), bf16[1,2,64,1152]{3,2,1,0:T(8,128)(2,1)}) %reduce-scatter.17.cloned.1.call-update) | async-done | bytes 294928 | tf_op jit(solution)/shard_map/reduce_scatter | solution.py:117
  115.4 15.1 %all-gather.9.cloned.1.call-done = bf16[1,2,256,1152]{3,2,1,0:T(8,128)(2,1)} async-done(((bf16[1,2,64,1152]{3,2,1,0:T(8,128)(2,1)}), bf16[1,2,256,1152]{3,2,1,0:T(8,128)(2,1)}) %all-gather.9.cloned.1.call-update) | async-done | bytes 1179664 | tf_op jit(solution)/shard_map/all_gather | solution.py:138
  130.5 5.4 %fusion.82 = f32[512,1152]{1,0:T(8,128)} fusion(bf16[512,1152]{1,0:T(8,128)(2,1)} %bitcast.179, bf16[1152,1152]{1,0:T(8,128)(2,1)} %param.12), kind=kOutput, calls=%fused_computation.116 | convolution fusion | flops 1358954496 | bytes 6193152 | tf_op jit(solution)/shard_map/dot_general | solution.py:40
  135.9 14.1 %all-gather.7.cloned.1.call-done = bf16[1,2,256,1152]{3,2,1,0:T(8,128)(2,1)} async-done(((bf16[1,2,64,1152]{3,2,1,0:T(8,128)(2,1)}), bf16[1,2,256,1152]{3,2,1,0:T(8,128)(2,1)}) %all-gather.7.cloned.1.call-update) | async-done | bytes 1179664 | tf_op jit(solution)/shard_map/all_gather | solution.py:126
  150.0 5.8 %fusion.16 = (bf16[512,1152]{1,0:T(8,128)(2,1)S(1)}, bf16[512,1152]{1,0:T(8,128)(2,1)}) fusion(f32[512,1152]{1,0:T(8,128)} %fusion.82, bf16[512,1152]{1,0:T(8,128)(2,1)} %bitcast.180, bf16[1152,1152]{1,0:T(8,128)(2,1)S(1)} %copy-done), kind=kOutput, calls=%fused_computation.26 | convolution fusion | flops 1371930624 | bytes 8552448 | tf_op jit(solution)/shard_map/dot_general | solution.py:34
  159.8 25.7 %reduce-scatter.21.cloned.1.call-done = bf16[1,2,64,1152]{3,2,1,0:T(8,128)(2,1)} async-done(((bf16[1,2,256,1152]{3,2,1,0:T(8,128)(2,1)}), bf16[1,2,64,1152]{3,2,1,0:T(8,128)(2,1)}) %reduce-scatter.21.cloned.1.call-update) | async-done | bytes 294928 | tf_op jit(solution)/shard_map/reduce_scatter | solution.py:143
  191.6 15.5 %all-gather.11.cloned.1.call-done = bf16[1,2,256,1152]{3,2,1,0:T(8,128)(2,1)} async-done(((bf16[1,2,64,1152]{3,2,1,0:T(8,128)(2,1)}), bf16[1,2,256,1152]{3,2,1,0:T(8,128)(2,1)}) %all-gather.11.cloned.1.call-update) | async-done | bytes 1179664 | tf_op jit(solution)/shard_map/all_gather | solution.py:153
  212.3 4.9 fusion.2
  217.2 5.0 fusion.3
  225.5 11.5 %all_to_all.62 = bf16[1,2,256,288]{3,1,0,2:T(2,128)(2,1)} all-to-all(bf16[1,2,256,288]{3,1,0,2:T(2,128)(2,1)} %copy.71), channel_id=1, replica_groups=mesh['dp'=4,'seq'=2,'tensor'=4] {'seq'}, dimensions={2} | all-to-all | bytes 589824 | tf_op jit(solution)/shard_map/all_to_all | solution.py:156
  253.9 15.1 %all_to_all.63 = bf16[1,4,128,864]{2,3,0,1:T(8,128)(2,1)S(1)} all-to-all(bf16[1,4,128,864]{2,3,0,1:T(8,128)(2,1)} %bitcast.166), channel_id=1, replica_groups=mesh['dp'=4,'seq'=2,'tensor'=4] {'seq'}, dimensions={1} | all-to-all | bytes 1769472 | tf_op jit(solution)/shard_map/all_to_all | solution.py:164
  284.2 4.8 convolution_convert_fusion
  289.1 5.1 fusion.6
  295.6 50.4 %reduce-scatter.33.cloned.1.call-done = bf16[1152,288]{0,1:T(8,128)(2,1)} async-done(((bf16[1152,1152]{0,1:T(8,128)(2,1)}), bf16[1152,288]{0,1:T(8,128)(2,1)}) %reduce-scatter.33.cloned.1.call-update) | async-done | bytes 663568 | tf_op jit(solution)/shard_map/reduce_scatter | solution.py:176
  346.0 27.6 %reduce-scatter.23.cloned.1.call-done = bf16[1,2,64,1152]{3,2,1,0:T(8,128)(2,1)} async-done(((bf16[1,2,256,1152]{3,2,1,0:T(8,128)(2,1)}), bf16[1,2,64,1152]{3,2,1,0:T(8,128)(2,1)}) %reduce-scatter.23.cloned.1.call-update) | async-done | bytes 294928 | tf_op jit(solution)/shard_map/reduce_scatter | solution.py:166
  375.4 53.3 %reduce-scatter.25.cloned.1.call-done = bf16[288,3,288]{2,0,1:T(8,128)(2,1)} async-done(((bf16[1152,3,288]{2,0,1:T(8,128)(2,1)}), bf16[288,3,288]{2,0,1:T(8,128)(2,1)}) %reduce-scatter.25.cloned.1.call-update) | async-done | bytes 497680 | tf_op jit(solution)/shard_map/reduce_scatter | solution.py:195
  431.1 25.2 %reduce-scatter.19.cloned.1.call-done = bf16[1,2,64,1152]{3,2,1,0:T(8,128)(2,1)} async-done(((bf16[1,2,256,1152]{3,2,1,0:T(8,128)(2,1)}), bf16[1,2,64,1152]{3,2,1,0:T(8,128)(2,1)}) %reduce-scatter.19.cloned.1.call-update) | async-done | bytes 294928 | tf_op jit(solution)/shard_map/reduce_scatter | solution.py:129
  458.9 11.6 %reduce-scatter.39.cloned.1.call-done = bf16[144,288]{1,0:T(8,128)(2,1)} async-done(((bf16[288,288]{1,0:T(8,128)(2,1)}), bf16[144,288]{1,0:T(8,128)(2,1)}) %reduce-scatter.39.cloned.1.call-update) | async-done | bytes 82960
  470.5 18.9 %reduce-scatter.31.cloned.1.call-done = bf16[144,1152]{1,0:T(8,128)(2,1)} async-done(((bf16[288,1152]{1,0:T(8,128)(2,1)}), bf16[144,1152]{1,0:T(8,128)(2,1)}) %reduce-scatter.31.cloned.1.call-update) | async-done | bytes 331792 | tf_op jit(solution)/shard_map/reduce_scatter | solution.py:200
  489.3 18.9 %reduce-scatter.35.cloned.1.call-done = bf16[1152,144]{0,1:T(8,128)(2,1)} async-done(((bf16[1152,288]{0,1:T(8,128)(2,1)}), bf16[1152,144]{0,1:T(8,128)(2,1)}) %reduce-scatter.35.cloned.1.call-update) | async-done | bytes 331792 | tf_op jit(solution)/shard_map/reduce_scatter | solution.py:184
  508.2 18.9 %reduce-scatter.27.cloned.1.call-done = bf16[144,3,288]{2,0,1:T(8,128)(2,1)} async-done(((bf16[288,3,288]{2,0,1:T(8,128)(2,1)}), bf16[144,3,288]{2,0,1:T(8,128)(2,1)}) %reduce-scatter.27.cloned.1.call-update) | async-done | bytes 248848 | tf_op jit(solution)/shard_map/reduce_scatter | solution.py:203
  (137 shorter events, 98.5 us)
Async XLA Ops:
  7.2 142.8 %copy-start = (bf16[1152,1152]{1,0:T(8,128)(2,1)S(1)}, bf16[1152,1152]{1,0:T(8,128)(2,1)}, u32[]{:S(2)}) copy-start(bf16[1152,1152]{1,0:T(8,128)(2,1)} %param.11) | copy-start | bytes 7962628
  7.2 26.2 %all-gather.5.cloned.1.call-start = ((), (), s32[]{:S(2)}) async-start(), calls=%async_computation.16 | async-start | bytes 1474560 | tf_op jit(solution)/shard_map/all_gather | solution.py:103
  8.8 28.8 %copy-start.11 = (f32[1152]{0:T(1024)}, f32[1152]{0:T(1024)S(1)}, u32[]{:S(2)}) copy-start(f32[1152]{0:T(1024)S(1)} %get-tuple-element.38) | copy-start | bytes 13828
  9.9 27.7 %copy-start.15 = (f32[2,64]{1,0:T(2,128)}, f32[2,64]{1,0:T(2,128)S(1)}, u32[]{:S(2)}) copy-start(f32[2,64]{1,0:T(2,128)S(1)} %broadcast_multiply_fusion.5) | copy-start | bytes 1540
  11.1 26.5 %copy-start.17 = (f32[2,64]{1,0:T(2,128)}, f32[2,64]{1,0:T(2,128)S(1)}, u32[]{:S(2)}) copy-start(f32[2,64]{1,0:T(2,128)S(1)} %add_rsqrt_fusion.1) | copy-start | bytes 1540
  13.1 97.9 %reduce-scatter.17.cloned.1.call-start = ((), (), s32[]{:S(2)}) async-start(), calls=%async_computation.17 | async-start | bytes 1474560 | tf_op jit(solution)/shard_map/reduce_scatter | solution.py:117
  83.0 28.0 %copy-start.1 = (bf16[1,2,64,1152]{3,2,1,0:T(8,128)(2,1)S(1)}, bf16[1,2,64,1152]{3,2,1,0:T(8,128)(2,1)}, u32[]{:S(2)}) copy-start(bf16[1,2,64,1152]{3,2,1,0:T(8,128)(2,1)} %param.7) | copy-start | bytes 884740
  86.1 27.2 %copy-start.14 = (f32[1152]{0:T(1024)S(1)}, f32[1152]{0:T(1024)}, u32[]{:S(2)}) copy-start(f32[1152]{0:T(1024)} %get-tuple-element.35) | copy-start | bytes 13828
  86.1 44.4 %all-gather.9.cloned.1.call-start = ((), (), s32[]{:S(2)}) async-start(), calls=%async_computation.20 | async-start | bytes 1474560 | tf_op jit(solution)/shard_map/all_gather | solution.py:138
  87.0 63.0 %all-gather.7.cloned.1.call-start = ((), (), s32[]{:S(2)}) async-start(), calls=%async_computation.18 | async-start | bytes 1474560 | tf_op jit(solution)/shard_map/all_gather | solution.py:126
  115.2 70.3 %reduce-scatter.21.cloned.1.call-start = ((), (), s32[]{:S(2)}) async-start(), calls=%async_computation.21 | async-start | bytes 1474560 | tf_op jit(solution)/shard_map/reduce_scatter | solution.py:143
  156.8 28.7 %copy-start.2 = (bf16[1,2,64,1152]{3,2,1,0:T(8,128)(2,1)S(1)}, bf16[1,2,64,1152]{3,2,1,0:T(8,128)(2,1)}, u32[]{:S(2)}) copy-start(bf16[1,2,64,1152]{3,2,1,0:T(8,128)(2,1)} %reduce-scatter.17.cloned.1.call-done) | copy-start | bytes 884740
  159.8 47.3 %all-gather.11.cloned.1.call-start = ((), (), s32[]{:S(2)}) async-start(), calls=%async_computation.22 | async-start | bytes 1474560 | tf_op jit(solution)/shard_map/all_gather | solution.py:153
  189.5 104.8 %reduce-scatter.37.cloned.1.call-start = ((), (), s32[]{:S(2)}) async-start(), calls=%async_computation.30 | async-start | bytes 1105920
  212.2 82.8 %reduce-scatter.29.cloned.1.call-start = ((), (), s32[]{:S(2)}) async-start(), calls=%async_computation.26 | async-start | bytes 3317760 | tf_op jit(solution)/shard_map/reduce_scatter | solution.py:192
  217.2 128.8 %reduce-scatter.33.cloned.1.call-start = ((), (), s32[]{:S(2)}) async-start(), calls=%async_computation.28 | async-start | bytes 3317760 | tf_op jit(solution)/shard_map/reduce_scatter | solution.py:176
  222.3 151.3 %reduce-scatter.23.cloned.1.call-start = ((), (), s32[]{:S(2)}) async-start(), calls=%async_computation.23 | async-start | bytes 1474560 | tf_op jit(solution)/shard_map/reduce_scatter | solution.py:166
  279.5 149.2 %reduce-scatter.25.cloned.1.call-start = ((), (), s32[]{:S(2)}) async-start(), calls=%async_computation.24 | async-start | bytes 3317760 | tf_op jit(solution)/shard_map/reduce_scatter | solution.py:195
  289.0 167.3 %reduce-scatter.19.cloned.1.call-start = ((), (), s32[]{:S(2)}) async-start(), calls=%async_computation.19 | async-start | bytes 1474560 | tf_op jit(solution)/shard_map/reduce_scatter | solution.py:129
  294.2 162.2 %copy-start.4 = (bf16[1,2,64,1152]{3,2,1,0:T(8,128)(2,1)S(1)}, bf16[1,2,64,1152]{3,2,1,0:T(8,128)(2,1)}, u32[]{:S(2)}) copy-start(bf16[1,2,64,1152]{3,2,1,0:T(8,128)(2,1)} %reduce-scatter.21.cloned.1.call-done) | copy-start | bytes 884740
  294.2 176.3 %reduce-scatter.39.cloned.1.call-start = ((), (), s32[]{:S(2)}) async-start(), calls=%async_computation.31 | async-start | bytes 331776
  294.9 194.4 %reduce-scatter.31.cloned.1.call-start = ((), (), s32[]{:S(2)}) async-start(), calls=%async_computation.27 | async-start | bytes 995328 | tf_op jit(solution)/shard_map/reduce_scatter | solution.py:200
  295.5 212.7 %reduce-scatter.35.cloned.1.call-start = ((), (), s32[]{:S(2)}) async-start(), calls=%async_computation.29 | async-start | bytes 995328 | tf_op jit(solution)/shard_map/reduce_scatter | solution.py:184
  346.0 181.1 %reduce-scatter.27.cloned.1.call-start = ((), (), s32[]{:S(2)}) async-start(), calls=%async_computation.25 | async-start | bytes 995328 | tf_op jit(solution)/shard_map/reduce_scatter | solution.py:203
  (16 other events, 73.4 us)
Sparse Core Ops, SparseCore 0:
  13.2 20.1 all-gather.4
  86.2 24.6 reduce-scatter.16
  113.1 17.4 all-gather.8
  132.5 17.4 all-gather.6
  159.9 25.5 reduce-scatter.20
  189.6 17.4 all-gather.10
  212.3 24.6 reduce-scatter.36
  239.4 51.8 reduce-scatter.28
  293.5 52.3 reduce-scatter.32
  348.3 25.1 reduce-scatter.22
  375.9 52.7 reduce-scatter.24
  431.1 25.1 reduce-scatter.18
  459.2 11.2 reduce-scatter.38
  473.1 16.1 reduce-scatter.30
  492.0 16.1 reduce-scatter.34
  510.9 16.1 reduce-scatter.26
where the time goes:
time: 535 us; the launch traced here: 534 us
  waiting for transfers between devices  341 us (64%)
  matrix products  61.5 us (11%)
  blocking collectives  50.8 us (9%)
  local copies, waits for them, and re-layouts  40.7 us (8%)
  other arithmetic  24.7 us (5%)
  between operations  14.2 us (3%)
    reduce_scatter x1, waiting for transfers between devices, body(): lax.psum_scatter(in_local.astype(jnp.bfloat16), 'dp', scatter_dimension=0...  53.3 us
    reduce_scatter x1, waiting for transfers between devices, body(): lax.psum_scatter(down_local.astype(jnp.bfloat16), 'dp', scatter_dimension...  50.4 us
    reduce_scatter x1, waiting for transfers between devices, body(): lax.psum_scatter(flat_dot_t(projected_grad, in_flat).astype(jnp.bfloat16)...  27.6 us
    reduce_scatter x1, waiting for transfers between devices, body(): lax.psum_scatter(flat_dot_t(hidden_grad, up_weight).astype(jnp.bfloat16),...  25.7 us
    reduce_scatter x1, waiting for transfers between devices, body(): lax.psum_scatter(flat_dot(activated, down_weight).astype(jnp.bfloat16), '...  25.2 us
    reduce_scatter x1, waiting for transfers between devices, body(): lax.psum_scatter(flat_dot(attended_rows, out_weight).astype(jnp.bfloat16)...  23.9 us
    all_gather x1, waiting for transfers between devices, body(): first_full = lax.all_gather(first_input, 'tensor', axis=2, tiled=True)  20.3 us
    reduce_scatter x1, waiting for transfers between devices, body(): lax.psum_scatter(row_groups[0].astype(jnp.bfloat16), 'seq', scatter_dimen...  18.9 us
  transfers between devices with their start and end apart: 16, of which 14 were waited for; matrix products, arithmetic and copies ran while one was open for 14% of the time, Pallas kernels for 0%

commit v1 on v0

v1 whole, which is shorter than its diff:
```python
import functools
import math

import jax
import jax.numpy as jnp
from jax import lax
from jax.experimental import pallas as pl
from jax.experimental.pallas import tpu as pltpu
from jax.sharding import PartitionSpec as P

HEAD_DIM = 72
epsilon = 1e-06
MESH = pl.DeviceIdType.MESH
F32 = jnp.float32
BF16 = jnp.bfloat16


def normalize(rows):
    center = jnp.mean(rows, axis=-1, keepdims=True)
    centred = rows - center
    spread = jnp.mean(centred * centred, axis=-1, keepdims=True)
    inverse = lax.rsqrt(spread + epsilon)
    return (centred * inverse, inverse)


def norm_back(normed, inverse, upstream):
    mean_grad = jnp.mean(upstream, axis=-1, keepdims=True)
    mean_cross = jnp.mean(upstream * normed, axis=-1, keepdims=True)
    return (upstream - mean_grad - normed * mean_cross) * inverse


def dot(left, right):
    return jnp.dot(left, right, preferred_element_type=F32)


def dot_t(left, right):
    return lax.dot_general(left, right, (((1,), (1,)), ((), ())), preferred_element_type=F32)


def head_sums(product, same_head):
    high = product.astype(BF16)
    low = (product - high.astype(F32)).astype(BF16)
    return dot(high, same_head) + dot(low, same_head)


def kernel(dims, lat, mod, in_w, out_w, up_w, down_w, cot, same_head,
           res_out, lgrad_out, gin_out, gout_out, gup_out, gdown_out,
           LAT, COT, FIRST, BRANCH, SECOND, ATTG, QKV, DQKV, ATT, DACT, ACT, HG, XT, PART, keep,
           MID, MIDG, RESB, RESR, LGB, LGR, rsA, rsB, rsC, rsD,
           gdown, gup, gout, gin, ssem, rsem):
    Z, S, T, Fl, Pb, D, H, K = dims
    O = T // 2
    Fr = Fl * S
    R = Fr * Pb
    N = T * R
    z, s, t = lax.axis_index("dp"), lax.axis_index("seq"), lax.axis_index("tensor")
    o, inner = t // 2, lax.rem(t, 2)
    partner = {"tensor": o * 2 + 1 - inner}

    def outer(k):
        return lax.rem(o + k, O)

    def seq_peer(k):
        return lax.rem(s + k, S)

    def dp_peer(k):
        return lax.rem(z + k, Z)

    sends = []

    def send(src, dst, device):
        i = len(sends)
        copy = pltpu.make_async_remote_copy(
            src_ref=src, dst_ref=dst, send_sem=ssem.at[i], recv_sem=rsem.at[i],
            device_id=device, device_id_type=MESH)
        copy.start()
        sends.append(copy)
        return copy

    barrier = pltpu.get_barrier_semaphore()
    peers = [partner]
    peers += [{"tensor": outer(k) * 2 + inner} for k in range(1, O)]
    peers += [{"seq": seq_peer(k)} for k in range(1, S)]
    peers += [{"dp": dp_peer(k)} for k in range(1, Z)]
    for peer in peers:
        pl.semaphore_signal(barrier, inc=1, device_id=peer, device_id_type=MESH)
    pl.semaphore_wait(barrier, len(peers))

    def row(i):
        return mod[i : i + 1, :]

    def exchange_in(src, dst):
        copies = []
        for k in range(1, S):
            p = seq_peer(k)
            copies.append(send(src.at[:, p], dst.at[pl.ds(s * Fl, Fl)], {"seq": p}))
        dst[pl.ds(s * Fl, Fl)] = src[:, s]
        return copies

    def exchange_out(src, landed):
        copies = []
        for k in range(1, S):
            p = seq_peer(k)
            copies.append(send(src.at[pl.ds(p * Fl, Fl)], landed.at[k - 1], {"seq": p}))
        return copies

    def exchange_end(src, landed, out, copies):
        out[:, s] = src[pl.ds(s * Fl, Fl)]
        for k in range(1, S):
            copies[k - 1].wait_recv()
            out[:, lax.rem(s + S - k, S)] = landed[k - 1]

    def gather_start(buf):
        far = [send(buf.at[t], buf.at[t], {"tensor": outer(k) * 2 + inner}) for k in range(1, O)]
        near = [send(buf.at[t], buf.at[t], partner)]
        return far, near

    def gather_end(buf, state):
        far, near = state
        for k in range(1, O):
            far[k - 1].wait_recv()
            slot = lax.rem(o + O - k, O) * 2 + inner
            near.append(send(buf.at[slot], buf.at[slot], partner))
        for copy in near:
            copy.wait_recv()

    def scatter_start(compute, bufs):
        send1, recv1, send2, recv2 = bufs
        first = {}
        for k in list(range(1, O)) + [0]:
            PART[...] = compute(outer(k)).reshape(2, R, D)
            send1[k] = PART[1 - inner].astype(BF16)
            first[k] = send(send1.at[k], recv1.at[k], partner)
            keep[k] = PART[inner]
        second = []
        for k in range(1, O):
            first[k].wait_recv()
            send2[k - 1] = (keep[k] + recv1[k].astype(F32)).astype(BF16)
            second.append(send(send2.at[k - 1], recv2.at[k - 1], {"tensor": outer(k) * 2 + inner}))
        return first[0], second

    def scatter_end(bufs, state):
        send1, recv1, send2, recv2 = bufs
        state[0].wait_recv()
        total = keep[0] + recv1[0].astype(F32)
        for k in range(1, O):
            state[1][k - 1].wait_recv()
            total = total + recv2[k - 1].astype(F32)
        return total

    def pair(buf, i):
        both = buf[pl.ds(2 * i, 2)]
        return both.reshape(2 * R, both.shape[-1])

    def put_pair(buf, i, value):
        buf[pl.ds(2 * i, 2)] = value.reshape(2, R, value.shape[-1])

    def over_pairs(fn):
        def step(i, carry):
            fn(i)
            return carry
        lax.fori_loop(0, O, step, 0)

    def transpose_of(buf):
        for i in range(T):
            block = buf[i].T
            XT[:, :, i * R : (i + 1) * R] = block.reshape(Z, D // Z, R)

    def weight_start(right, bufs):
        local, rx, pz, rz = bufs
        def step(i, carry):
            value = dot(XT[i], right()).astype(BF16)
            local[i] = value.reshape(S, D // (Z * S), value.shape[-1])
            return carry
        lax.fori_loop(0, Z, step, 0)
        return [send(local.at[:, seq_peer(k)], rx.at[k - 1], {"seq": seq_peer(k)})
                for k in range(1, S)]

    def weight_mid(bufs, copies):
        local, rx, pz, rz = bufs
        for copy in copies:
            copy.wait_recv()
        def step(i, carry):
            total = local[i, s].astype(F32)
            for k in range(1, S):
                total = total + rx[k - 1, i].astype(F32)
            pz[i] = total.astype(BF16)
            return carry
        lax.fori_loop(0, Z, step, 0)
        return [send(pz.at[dp_peer(k)], rz.at[k - 1], {"dp": dp_peer(k)}) for k in range(1, Z)]

    def weight_end(bufs, copies):
        local, rx, pz, rz = bufs
        total = pz[z].astype(F32)
        for k in range(1, Z):
            copies[k - 1].wait_recv()
            total = total + rz[k - 1].astype(F32)
        return total.astype(BF16)

    lat_in = exchange_in(lat, LAT)
    cot_in = exchange_in(cot, COT)
    for copy in lat_in:
        copy.wait_recv()
    inputs = LAT[...].reshape(R, D).astype(F32)
    first_normed, first_inverse = normalize(inputs)
    FIRST[t] = (first_normed * (1.0 + row(1)) + row(0)).astype(BF16)
    first_state = gather_start(FIRST)
    for copy in cot_in:
        copy.wait_recv()
    BRANCH[t] = (row(5) * COT[...].reshape(R, D).astype(F32)).astype(BF16)
    branch_state = gather_start(BRANCH)
    gather_end(FIRST, first_state)

    def project(i):
        rows = pair(FIRST, i)
        for j in range(3):
            put_pair(QKV.at[j], i, dot(rows, in_w[j]).astype(BF16))
    over_pairs(project)

    scaling = 1.0 / math.sqrt(HEAD_DIM)

    def part(buf, j, i):
        return buf[j, i].astype(F32).reshape(Fr, Pb, H)

    def probabilities(q, k):
        scores = [head_sums((q * k[g : g + 1]).reshape(R, H), same_head[...]) * scaling for g in range(Fr)]
        highest = functools.reduce(jnp.maximum, scores)
        raised = [jnp.exp(score - highest) for score in scores]
        total = functools.reduce(jnp.add, raised)
        return [value / total for value in raised]

    def low(value):
        return value.astype(BF16).astype(F32)

    def attention(i, carry):
        q, k, v = part(QKV, 0, i), part(QKV, 1, i), part(QKV, 2, i)
        probs = probabilities(q, k)
        total = jnp.zeros((Fr, Pb, H), F32)
        for g in range(Fr):
            total = total + low(probs[g]).reshape(Fr, Pb, H) * v[g : g + 1]
        ATT[i] = total.reshape(R, H).astype(BF16)
        return carry
    lax.fori_loop(0, T, attention, 0)

    att_state = scatter_start(lambda i: dot(pair(ATT, i), out_w[...]), rsA)
    gather_end(BRANCH, branch_state)

    def branch_back(i):
        put_pair(DACT, i, dot_t(pair(BRANCH, i), down_w[...]))
    over_pairs(branch_back)
    midway = LAT[...].reshape(R, D).astype(F32) + row(2) * scatter_end(rsA, att_state)
    MID[...] = midway
    second_normed, second_inverse = normalize(midway)
    SECOND[t] = (second_normed * (1.0 + row(4)) + row(3)).astype(BF16)
    second_state = gather_start(SECOND)
    transpose_of(BRANCH)
    gather_end(SECOND, second_state)

    c = math.sqrt(2.0 / math.pi)

    def mlp(i):
        hidden = dot(pair(SECOND, i), up_w[...])
        square = hidden * hidden
        curve = jnp.tanh(c * (hidden + 0.044715 * square * hidden))
        put_pair(ACT, i, (0.5 * hidden * (1.0 + curve)).astype(BF16))
        slope = 0.5 * (1.0 + curve) + 0.5 * hidden * (1.0 - curve * curve) * (c * (1.0 + 3 * 0.044715 * square))
        put_pair(HG, i, (pair(DACT, i) * slope).astype(BF16))
    over_pairs(mlp)

    second_grad_state = scatter_start(lambda i: dot_t(pair(HG, i), up_w[...]), rsB)
    down_x = weight_start(lambda: ACT[...].reshape(N, K), gdown)
    second_grad = scatter_end(rsB, second_grad_state)
    second_normed, second_inverse = normalize(MID[...])
    midway_grad = COT[...].reshape(R, D).astype(F32) + norm_back(
        second_normed, second_inverse, second_grad * (1.0 + row(4)))
    MIDG[...] = midway_grad
    ATTG[t] = (row(2) * midway_grad).astype(BF16)
    attg_state = gather_start(ATTG)
    transpose_of(SECOND)
    up_x = weight_start(lambda: HG[...].reshape(N, K), gup)
    gather_end(ATTG, attg_state)

    def attention_back(i, carry):
        q, k, v = part(QKV, 0, i), part(QKV, 1, i), part(QKV, 2, i)
        grad = dot_t(ATTG[i], out_w[...]).astype(BF16).astype(F32).reshape(Fr, Pb, H)
        probs = probabilities(q, k)
        prob_grads = [head_sums((grad * v[g : g + 1]).reshape(R, H), same_head[...]) for g in range(Fr)]
        cross = functools.reduce(jnp.add, [a * b for a, b in zip(probs, prob_grads)])
        dq = jnp.zeros((Fr, Pb, H), F32)
        for g in range(Fr):
            score = low(probs[g] * (prob_grads[g] - cross) * scaling).reshape(Fr, Pb, H)
            dq = dq + score * k[g : g + 1]
            DQKV[1, i, g * Pb : (g + 1) * Pb] = jnp.sum(score * q, axis=0).astype(BF16)
            DQKV[2, i, g * Pb : (g + 1) * Pb] = jnp.sum(
                low(probs[g]).reshape(Fr, Pb, H) * grad, axis=0).astype(BF16)
        DQKV[0, i] = dq.reshape(R, H).astype(BF16)
        return carry
    lax.fori_loop(0, T, attention_back, 0)

    def first_back(i):
        return sum(dot_t(pair(DQKV.at[j], i), in_w[j]) for j in range(3))
    first_grad_state = scatter_start(first_back, rsC)
    transpose_of(FIRST)
    in_x = [weight_start(lambda j=j: DQKV[j].reshape(N, H), gin[j]) for j in range(3)]
    first_grad = scatter_end(rsC, first_grad_state)
    first_normed, first_inverse = normalize(LAT[...].reshape(R, D).astype(F32))
    LGB[...] = (MIDG[...] + norm_back(first_normed, first_inverse, first_grad * (1.0 + row(1)))
                ).astype(BF16).reshape(Fr, Pb, D)
    lgrad_copies = exchange_out(LGB, LGR)

    result_state = scatter_start(lambda i: dot(pair(ACT, i), down_w[...]), rsD)
    transpose_of(ATTG)
    out_x = weight_start(lambda: ATT[...].reshape(N, H), gout)
    down_z = weight_mid(gdown, down_x)
    feedforward = scatter_end(rsD, result_state)
    RESB[...] = (MID[...] + row(5) * feedforward).astype(BF16).reshape(Fr, Pb, D)
    res_copies = exchange_out(RESB, RESR)
    up_z = weight_mid(gup, up_x)
    in_z = [weight_mid(gin[j], in_x[j]) for j in range(3)]
    exchange_end(LGB, LGR, lgrad_out, lgrad_copies)
    out_z = weight_mid(gout, out_x)
    exchange_end(RESB, RESR, res_out, res_copies)
    gdown_out[...] = weight_end(gdown, down_z)
    gup_out[...] = weight_end(gup, up_z)
    for j in range(3):
        gin_out[j] = weight_end(gin[j], in_z[j])
    gout_out[...] = weight_end(gout, out_z)
    for copy in sends:
        copy.wait_send()


def body(sizes, latents, modulation, in_weight, out_weight, up_weight, down_weight, cotangent):
    Z, S, T = sizes
    _, Fl, Pl, D = latents.shape
    H, K = out_weight.shape[0], up_weight.shape[1]
    Pb, O = Pl // S, T // 2
    Fr = Fl * S
    R = Fr * Pb
    chunk = D // (Z * S)
    heads = jnp.arange(H) // HEAD_DIM
    same_head = (heads[:, None] == heads[None, :]).astype(BF16)

    def scatter_bufs():
        return (pltpu.VMEM((O, R, D), BF16), pltpu.VMEM((O, R, D), BF16),
                pltpu.VMEM((O - 1, R, D), BF16), pltpu.VMEM((O - 1, R, D), BF16))

    def weight_bufs(cols):
        return (pltpu.VMEM((Z, S, chunk, cols), BF16), pltpu.VMEM((S - 1, Z, chunk, cols), BF16),
                pltpu.VMEM((Z, chunk, cols), BF16), pltpu.VMEM((Z - 1, chunk, cols), BF16))

    full = pltpu.VMEM((T, R, D), BF16)
    tokens = pltpu.VMEM((Fr, Pb, D), BF16)
    landed = pltpu.VMEM((S - 1, Fl, Pb, D), BF16)
    copies = 2 * 4 * (S - 1 + O) + 4 * 2 * O + 6 * (S + Z)
    scratch = [
        tokens, tokens, full, full, full, full,
        pltpu.VMEM((3, T, R, H), BF16), pltpu.VMEM((3, T, R, H), BF16),
        pltpu.VMEM((T, R, H), BF16), pltpu.VMEM((T, R, K), F32),
        pltpu.VMEM((T, R, K), BF16), pltpu.VMEM((T, R, K), BF16),
        pltpu.VMEM((Z, D // Z, T * R), BF16), pltpu.VMEM((2, R, D), F32),
        pltpu.VMEM((O, R, D), F32),
        pltpu.VMEM((R, D), F32), pltpu.VMEM((R, D), F32),
        tokens, landed, tokens, landed,
        scatter_bufs(), scatter_bufs(), scatter_bufs(), scatter_bufs(),
        weight_bufs(K), weight_bufs(K), weight_bufs(H), tuple(weight_bufs(H) for _ in range(3)),
        pltpu.SemaphoreType.DMA((copies,)), pltpu.SemaphoreType.DMA((copies,)),
    ]
    vmem = pl.BlockSpec(memory_space=pltpu.VMEM)
    shape = jax.ShapeDtypeStruct
    outs = pl.pallas_call(
        functools.partial(kernel, (Z, S, T, Fl, Pb, D, H, K)),
        out_shape=(
            shape((Fl, S, Pb, D), BF16), shape((Fl, S, Pb, D), BF16),
            shape((3, chunk, H), BF16), shape((chunk, H), BF16),
            shape((chunk, K), BF16), shape((chunk, K), BF16)),
        in_specs=[vmem] * 8,
        out_specs=(vmem,) * 6,
        scratch_shapes=scratch,
        compiler_params=pltpu.CompilerParams(
            collective_id=0, has_side_effects=True, vmem_limit_bytes=67043328),
    )(latents.reshape(Fl, S, Pb, D), modulation[0], in_weight.transpose(1, 0, 2), out_weight,
      up_weight, down_weight, cotangent.reshape(Fl, S, Pb, D), same_head)
    res, lgrad, gin, gout, gup, gdown = outs
    return (res.reshape(1, Fl, Pl, D), lgrad.reshape(1, Fl, Pl, D), gin.transpose(1, 0, 2),
            gout.T, gup, gdown.T)


def solution(mesh):
    placed = (
        P("dp", "seq", "tensor", None),
        P("dp", None, None),
        P(None, None, "tensor"),
        P("tensor", None),
        P(None, "tensor"),
        P("tensor", None),
        P("dp", "seq", "tensor", None),
    )
    sizes = (mesh.shape["dp"], mesh.shape["seq"], mesh.shape["tensor"])
    return jax.shard_map(
        functools.partial(body, sizes),
        mesh=mesh,
        in_specs=placed,
        out_specs=(
            P("dp", "seq", "tensor", None),
            P("dp", "seq", "tensor", None),
            P(("dp", "seq"), None, "tensor"),
            P("tensor", ("dp", "seq")),
            P(("dp", "seq"), "tensor"),
            P("tensor", ("dp", "seq")),
        ),
        check_vma=False,
    )
```

time: 535 us -> 210 us (0.39)
  waiting for transfers between devices: 341 us -> 0 us
  Pallas kernels: 0 us -> 193 us
  matrix products: 61.5 us -> 0 us
  blocking collectives: 50.8 us -> 0 us
  local copies, waits for them, and re-layouts: 40.7 us -> 14.7 us
  other arithmetic: 24.7 us -> 0.8 us
  between operations: 14.2 us -> 0.66 us
    reduce_scatter x10 -> x0, waiting for transfers between devices: 263 us -> none  [the longest x1 53.3 us: body(): lax.psum_scatter(in_local.astype(jnp.bfloat16), 'dp', scatter_dimension=0...]
    pallas_call x0 -> x1, Pallas kernels: none -> 193 us  [body(): pl.pallas_call(functools.partial(kernel, (Z, S, T, Fl, Pb, D, H, K)), out...]
    all_gather x4 -> x0, waiting for transfers between devices: 64.9 us -> none  [the longest x1 20.3 us: body(): first_full = lax.all_gather(first_input, 'tensor', axis=2, tiled=True)]
    dot_general x17 -> x0, matrix products: 57.4 us -> none  [the longest x4 18.2 us: flat_dot(): jnp.dot(left.reshape(-1, left.shape[-1]), right, preferred_element_type=j...]
    all_to_all x4 -> x0, blocking collectives: 50.8 us -> none  [the longest x1 16.4 us: body(): lax.all_to_all(projected, 'seq', split_axis=2, concat_axis=1, tiled=True)]
    unnamed x18 -> x0, waiting for transfers between devices: 13 us -> none
    all_to_all x8 -> x0, local copies, waits for them, and re-layouts: 12.8 us -> none  [the longest x2 4.08 us: body(): lax.all_to_all(stacked_grad, 'seq', split_axis=1, concat_axis=2, tiled=True)]
    convert_element_type x5 -> x1, other arithmetic: 9.19 us -> 0.79 us  [body(): same_head = (heads[:, None] == heads[None, :]).astype(BF16)]
  transfers between devices with their start and end apart: 16 -> 0, of which waited for: 14 -> 0; matrix products, arithmetic and copies ran while one was open for 14% -> 0% of each run, Pallas kernels for 0% -> 0%
where the time goes in v1:
time: 210 us
  Pallas kernels  193 us (92%)
  local copies, waits for them, and re-layouts  14.7 us (7%)
    pallas_call x1, Pallas kernels, body(): pl.pallas_call(functools.partial(kernel, (Z, S, T, Fl, Pb, D, H, K)), out...  193 us
    unnamed x10, local copies, waits for them, and re-layouts  14.7 us

profile of v1, /device:TPU:0, one launch (start us, length us, event | category | flops | bytes accessed | tf_op | source)
XLA Modules:
  0.0 209.5 jit_solution(968962474604080395)
XLA Ops:
  0.6 1.4 copy.16
  2.0 0.8 compare_convert_fusion.same_head
  2.8 4.2 %copy.13 = bf16[1152,3,288]{2,0,1:T(8,128)(2,1)} copy(bf16[1152,3,288]{0,2,1:T(8,128)(2,1)} %param.9) | data formatting | bytes 3981312 | tf_op args[2]
  7.0 193.3 %shard_map.118 = (bf16[2,2,32,1152]{3,2,1,0:T(8,128)(2,1)}, bf16[2,2,32,1152]{3,2,1,0:T(8,128)(2,1)}, bf16[3,144,288]{2,1,0:T(8,128)(2,1)}, bf16[144,288]{1,0:T(...) custom-call(bf16[2,2,32,1152]{3,2,1,0:T(8,128)(2,1)} %bitcast.14, f32[6,1152]{1,0:T(8,128)} %bitcast.18, ...), custom_call_target="tpu_custom_call" | custom-call | tf_op jit(solution)/shard_map/pallas_call | solution.py:370
  200.3 0.0 copy-start
  200.3 1.7 copy.23
  202.1 1.7 copy.24
  203.8 1.7 copy.25
  205.5 1.6 copy.26
  207.1 1.7 copy.27
  208.8 0.0 copy-done
  208.8 0.7 copy.28
  (1 shorter events, 0.0 us)
Async XLA Ops:
  200.3 8.5 %copy-start = (bf16[144,1152]{1,0:T(8,128)(2,1)S(1)}, bf16[144,1152]{1,0:T(8,128)(2,1)}, u32[]{:S(2)}) copy-start(bf16[144,1152]{1,0:T(8,128)(2,1)} %get-tuple-element.17) | copy-start | bytes 995332

commit v2 on v1

--- a/solution.py
+++ b/solution.py
@@ -279,6 +279,9 @@
     transpose_of(SECOND)
     up_x = weight_start(lambda: HG[...].reshape(N, K), gup)
     gather_end(ATTG, attg_state)
+    transpose_of(ATTG)
+    out_x = weight_start(lambda: ATT[...].reshape(N, H), gout)
+    down_z = weight_mid(gdown, down_x)
 
     def attention_back(i, carry):
         q, k, v = part(QKV, 0, i), part(QKV, 1, i), part(QKV, 2, i)
@@ -302,6 +305,8 @@
     first_grad_state = scatter_start(first_back, rsC)
     transpose_of(FIRST)
     in_x = [weight_start(lambda j=j: DQKV[j].reshape(N, H), gin[j]) for j in range(3)]
+    up_z = weight_mid(gup, up_x)
+    out_z = weight_mid(gout, out_x)
     first_grad = scatter_end(rsC, first_grad_state)
     first_normed, first_inverse = normalize(LAT[...].reshape(R, D).astype(F32))
     LGB[...] = (MIDG[...] + norm_back(first_normed, first_inverse, first_grad * (1.0 + row(1)))
@@ -309,16 +314,11 @@
     lgrad_copies = exchange_out(LGB, LGR)
 
     result_state = scatter_start(lambda i: dot(pair(ACT, i), down_w[...]), rsD)
-    transpose_of(ATTG)
-    out_x = weight_start(lambda: ATT[...].reshape(N, H), gout)
-    down_z = weight_mid(gdown, down_x)
+    in_z = [weight_mid(gin[j], in_x[j]) for j in range(3)]
     feedforward = scatter_end(rsD, result_state)
     RESB[...] = (MID[...] + row(5) * feedforward).astype(BF16).reshape(Fr, Pb, D)
     res_copies = exchange_out(RESB, RESR)
-    up_z = weight_mid(gup, up_x)
-    in_z = [weight_mid(gin[j], in_x[j]) for j in range(3)]
     exchange_end(LGB, LGR, lgrad_out, lgrad_copies)
-    out_z = weight_mid(gout, out_x)
     exchange_end(RESB, RESR, res_out, res_copies)
     gdown_out[...] = weight_end(gdown, down_z)
     gup_out[...] = weight_end(gup, up_z)

time: 210 us -> 202 us (0.962)
  Pallas kernels: 193 us -> 186 us
    pallas_call x1, Pallas kernels: 193 us -> 186 us  [body(): pl.pallas_call(functools.partial(kernel, (Z, S, T, Fl, Pb, D, H, K)), out...]
where the time goes in v2:
time: 202 us
  Pallas kernels  186 us (92%)
  local copies, waits for them, and re-layouts  14.7 us (7%)
    pallas_call x1, Pallas kernels, body(): pl.pallas_call(functools.partial(kernel, (Z, S, T, Fl, Pb, D, H, K)), out...  186 us
    unnamed x10, local copies, waits for them, and re-layouts  14.7 us

profile of v2, /device:TPU:0, one launch (start us, length us, event | category | flops | bytes accessed | tf_op | source)
XLA Modules:
  0.0 201.7 jit_solution(15212977808395333182)
XLA Ops:
  0.6 1.4 copy.16
  2.0 0.8 compare_convert_fusion.same_head
  2.8 4.2 %copy.13 = bf16[1152,3,288]{2,0,1:T(8,128)(2,1)} copy(bf16[1152,3,288]{0,2,1:T(8,128)(2,1)} %param.9) | data formatting | bytes 3981312 | tf_op args[2]
  7.0 185.6 %shard_map.118 = (bf16[2,2,32,1152]{3,2,1,0:T(8,128)(2,1)}, bf16[2,2,32,1152]{3,2,1,0:T(8,128)(2,1)}, bf16[3,144,288]{2,1,0:T(8,128)(2,1)}, bf16[144,288]{1,0:T(...) custom-call(bf16[2,2,32,1152]{3,2,1,0:T(8,128)(2,1)} %bitcast.14, f32[6,1152]{1,0:T(8,128)} %bitcast.18, ...), custom_call_target="tpu_custom_call" | custom-call | tf_op jit(solution)/shard_map/pallas_call | solution.py:370
  192.6 0.0 copy-start
  192.6 1.7 copy.23
  194.3 1.7 copy.24
  196.0 1.7 copy.25
  197.7 1.6 copy.26
  199.3 1.7 copy.27
  201.0 0.0 copy-done
  201.0 0.7 copy.28
  (1 shorter events, 0.0 us)
Async XLA Ops:
  192.6 8.5 %copy-start = (bf16[144,1152]{1,0:T(8,128)(2,1)S(1)}, bf16[144,1152]{1,0:T(8,128)(2,1)}, u32[]{:S(2)}) copy-start(bf16[144,1152]{1,0:T(8,128)(2,1)} %get-tuple-element.17) | copy-start | bytes 995332
